TPU v7x, 32 devices: a whole 2x2x4 slice. The times are simulated.
32 devices in a mesh: grp: 2 (over y), col: 4 (over z), slc: 2 (over x), bat: 2 (over core).
Axes of the slice: x: 2, y: 2, z: 4, core: 2. Of those that a mesh axis runs over, the one named last changes fastest.
Arguments:
- site_tensors: bfloat16 [4, 72, 2, 64, 128], P(('grp', 'slc'), 'col'), parts along dimension 0, may hold values from -1.2 to 1.2
- left_edge: float32 [4, 64, 128], P(('grp', 'slc')), parts along dimension 0, may hold values from -0.5 to 0.5
- right_edge: float32 [4, 64, 128], P(('grp', 'slc')), parts along dimension 0, may hold values from -0.5 to 0.5
- order: int32 [144], P(('grp', 'col')), parts along dimension 0, may hold values from 0 to 71, each once
- bitstrings: int32 [128, 72], P(('grp', 'bat')), parts along dimension 0, may hold values 0 or 1
Outputs:
- amplitudes: float32 [2, 128], P(None, ('grp', 'bat')), parts along dimension 1
There are 2 independent parts, one for each index of `grp`. A program takes and returns all parts, laid end to end along the dimension named above; each array names one. Nothing has to cross between parts.
Inputs may be any that keep to these rules, and one draw needn't show every extreme that they name: `order`: a permutation of the 72 qubit indices.
All inputs are finite; a program needn't handle non-finite values. No bound on the sum of `bitstrings` on one device may be relied on, other than what follows from the above.
Results may differ from a plain program's by a relative error of at most 0.0003.
Values sent between devices are 32-bit elements; how exact they have to be, the bound alone decides.
A program may use at most 64 MiB of HBM per device.

v0:
```python
import jax
import jax.numpy as jnp
from jax import lax
from jax.sharding import PartitionSpec as P


def rotate(block):
    middle = block.shape[-1] // 2
    return jnp.concatenate([-block[..., middle:], block[..., :middle]], axis=-1)


def complex_product(first_factor, second_factor):
    stacked = jnp.concatenate([second_factor, rotate(second_factor)], axis=-2)
    return jnp.einsum("bij,bjk->bik", first_factor, stacked, precision=lax.Precision.HIGHEST)


def closing(boundary, edge):
    middle = boundary.shape[-1] // 2
    real_left = boundary[..., :middle]
    imag_left = boundary[..., middle:]
    real_right = edge[..., :middle]
    imag_right = edge[..., middle:]
    real_part = jnp.sum(real_left * real_right - imag_left * imag_right, axis=(1, 2))
    imag_part = jnp.sum(real_left * imag_right + imag_left * real_right, axis=(1, 2))
    return jnp.stack([real_part, imag_part])


def select_site(tensors, site_bits, position):
    matrices = lax.dynamic_index_in_dim(tensors, position, 0, keepdims=False)
    chosen_bits = lax.dynamic_index_in_dim(site_bits, position, 1, keepdims=False)
    return jnp.where(chosen_bits[:, None, None] == 1, matrices[1], matrices[0])


def column_product(tensors, site_bits):
    site_count = tensors.shape[0]
    leading = select_site(tensors, site_bits, 0)
    return lax.fori_loop(
        1,
        site_count,
        lambda position, carried: complex_product(
            carried, select_site(tensors, site_bits, position)
        ),
        leading,
    )


def on_device(site_tensors, left_edge, right_edge, order, bitstrings):
    col_count = lax.axis_size("col")
    col_index = lax.axis_index("col")
    tensors = site_tensors[0].astype(jnp.float32)
    site_bits = jnp.take(bitstrings, order, axis=1)
    batch_rows = site_bits.shape[0]
    bond_size = left_edge.shape[1]
    product = column_product(tensors, site_bits)
    share = (batch_rows + col_count - 1) // col_count
    padded_rows = share * col_count
    grouped = product.reshape(col_count, share, bond_size, 2 * bond_size)
    received = lax.all_to_all(grouped, "col", split_axis=0, concat_axis=0, tiled=True)
    items = received.shape[1]
    start = jnp.broadcast_to(left_edge[0], (items, bond_size, 2 * bond_size))
    final_state = lax.fori_loop(
        0,
        received.shape[0],
        lambda position, carried: complex_product(
            carried, lax.dynamic_index_in_dim(received, position, 0, keepdims=False)
        ),
        start,
    )
    closed = closing(final_state, right_edge[0])
    placed = lax.dynamic_update_slice(
        jnp.zeros((2, padded_rows), jnp.float32), closed, (jnp.int32(0), col_index * share)
    )
    return lax.psum(placed, ("col", "slc"))


def solution(mesh):
    return jax.shard_map(
        on_device,
        mesh=mesh,
        in_specs=(
            P(("grp", "slc"), "col", None, None, None),
            P(("grp", "slc"), None, None),
            P(("grp", "slc"), None, None),
            P(("grp", "col")),
            P(("grp", "bat"), None),
        ),
        out_specs=P(None, ("grp", "bat")),
        check_vma=False,
    )
```

profile of v0, /device:TPU:0, one launch (start us, length us, event | category | flops | bytes accessed | tf_op | source)
XLA Modules:
  0.0 143.9 jit_solution(12536998118196753343)
XLA Ops:
  0.0 0.7 compare_select_fusion
  0.7 0.7 compare_and_fusion
  1.3 1.2 bitcast_convert_fusion
  2.6 0.6 gather_fusion
  3.3 1.1 broadcast_select_fusion.1
  4.4 83.2 %while.28 = (s32[]{:T(128)}, f32[32,64,128]{2,1,0:T(8,128)}, s32[32,18]{0,1:T(8,128)S(1)}, f32[18,2,64,128]{3,2,1,0:T(8,128)S(1)}, s32[]{:T(128)}, /*index=5*/s32[]{:T(128)}, s32[]{:T(128)}, s32[]{}) while((s32[]{:T(128)}, f32[32,64,128]{2,1,0:T(8,128)}, s32[32,18]{0,1:T(8,128)S(1)}, f32[18,2,64,128]{3,2,1,0:T(8,128)S(1)}, s32[]{:T(128)}, ...), condition=%wide.region_1.2_spmd, body=%wide.region_0.1_spmd.sunk | while | flops 404095008 | bytes 9634135 | solution.py:37
  4.9 1.2 copy.22
  6.2 3.1 %fusion.26 = f32[32,64,128]{2,1,0:T(8,128)} fusion(f32[32,64,128]{2,1,0:T(8,128)S(1)} %copy.22, f32[32,64,64]{2,1,0:T(8,128)S(1)} %get-tuple-element.256, f32[32,64,64]{2,1,0:T(8,128)S(1)} %get-tuple-element.257, f32[32,64,128]{2,1,0:T(8,128)S(1)} %broadcast_select_fusion.3), kind=kOutput, calls=%fused_computation.7.clone.1 | convolution fusion | flops 403701760 | bytes 4194304 | tf_op jit(solution)/shard_map/while/body/eval_jaxpr/bij,bjk->bik/dot_general | solution.py:14
  9.8 1.2 copy.22
  11.1 3.1 %fusion.26 = f32[32,64,128]{2,1,0:T(8,128)} fusion(f32[32,64,128]{2,1,0:T(8,128)S(1)} %copy.22, f32[32,64,64]{2,1,0:T(8,128)S(1)} %get-tuple-element.256, f32[32,64,64]{2,1,0:T(8,128)S(1)} %get-tuple-element.257, f32[32,64,128]{2,1,0:T(8,128)S(1)} %broadcast_select_fusion.3), kind=kOutput, calls=%fused_computation.7.clone.1 | convolution fusion | flops 403701760 | bytes 4194304 | tf_op jit(solution)/shard_map/while/body/eval_jaxpr/bij,bjk->bik/dot_general | solution.py:14
  14.7 1.2 copy.22
  16.0 3.1 %fusion.26 = f32[32,64,128]{2,1,0:T(8,128)} fusion(f32[32,64,128]{2,1,0:T(8,128)S(1)} %copy.22, f32[32,64,64]{2,1,0:T(8,128)S(1)} %get-tuple-element.256, f32[32,64,64]{2,1,0:T(8,128)S(1)} %get-tuple-element.257, f32[32,64,128]{2,1,0:T(8,128)S(1)} %broadcast_select_fusion.3), kind=kOutput, calls=%fused_computation.7.clone.1 | convolution fusion | flops 403701760 | bytes 4194304 | tf_op jit(solution)/shard_map/while/body/eval_jaxpr/bij,bjk->bik/dot_general | solution.py:14
  19.6 1.2 copy.22
  20.9 3.1 %fusion.26 = f32[32,64,128]{2,1,0:T(8,128)} fusion(f32[32,64,128]{2,1,0:T(8,128)S(1)} %copy.22, f32[32,64,64]{2,1,0:T(8,128)S(1)} %get-tuple-element.256, f32[32,64,64]{2,1,0:T(8,128)S(1)} %get-tuple-element.257, f32[32,64,128]{2,1,0:T(8,128)S(1)} %broadcast_select_fusion.3), kind=kOutput, calls=%fused_computation.7.clone.1 | convolution fusion | flops 403701760 | bytes 4194304 | tf_op jit(solution)/shard_map/while/body/eval_jaxpr/bij,bjk->bik/dot_general | solution.py:14
  24.5 1.2 copy.22
  25.8 3.1 %fusion.26 = f32[32,64,128]{2,1,0:T(8,128)} fusion(f32[32,64,128]{2,1,0:T(8,128)S(1)} %copy.22, f32[32,64,64]{2,1,0:T(8,128)S(1)} %get-tuple-element.256, f32[32,64,64]{2,1,0:T(8,128)S(1)} %get-tuple-element.257, f32[32,64,128]{2,1,0:T(8,128)S(1)} %broadcast_select_fusion.3), kind=kOutput, calls=%fused_computation.7.clone.1 | convolution fusion | flops 403701760 | bytes 4194304 | tf_op jit(solution)/shard_map/while/body/eval_jaxpr/bij,bjk->bik/dot_general | solution.py:14
  29.4 1.2 copy.22
  30.7 3.1 %fusion.26 = f32[32,64,128]{2,1,0:T(8,128)} fusion(f32[32,64,128]{2,1,0:T(8,128)S(1)} %copy.22, f32[32,64,64]{2,1,0:T(8,128)S(1)} %get-tuple-element.256, f32[32,64,64]{2,1,0:T(8,128)S(1)} %get-tuple-element.257, f32[32,64,128]{2,1,0:T(8,128)S(1)} %broadcast_select_fusion.3), kind=kOutput, calls=%fused_computation.7.clone.1 | convolution fusion | flops 403701760 | bytes 4194304 | tf_op jit(solution)/shard_map/while/body/eval_jaxpr/bij,bjk->bik/dot_general | solution.py:14
  34.3 1.2 copy.22
  35.5 3.1 %fusion.26 = f32[32,64,128]{2,1,0:T(8,128)} fusion(f32[32,64,128]{2,1,0:T(8,128)S(1)} %copy.22, f32[32,64,64]{2,1,0:T(8,128)S(1)} %get-tuple-element.256, f32[32,64,64]{2,1,0:T(8,128)S(1)} %get-tuple-element.257, f32[32,64,128]{2,1,0:T(8,128)S(1)} %broadcast_select_fusion.3), kind=kOutput, calls=%fused_computation.7.clone.1 | convolution fusion | flops 403701760 | bytes 4194304 | tf_op jit(solution)/shard_map/while/body/eval_jaxpr/bij,bjk->bik/dot_general | solution.py:14
  39.2 1.2 copy.22
  40.4 3.1 %fusion.26 = f32[32,64,128]{2,1,0:T(8,128)} fusion(f32[32,64,128]{2,1,0:T(8,128)S(1)} %copy.22, f32[32,64,64]{2,1,0:T(8,128)S(1)} %get-tuple-element.256, f32[32,64,64]{2,1,0:T(8,128)S(1)} %get-tuple-element.257, f32[32,64,128]{2,1,0:T(8,128)S(1)} %broadcast_select_fusion.3), kind=kOutput, calls=%fused_computation.7.clone.1 | convolution fusion | flops 403701760 | bytes 4194304 | tf_op jit(solution)/shard_map/while/body/eval_jaxpr/bij,bjk->bik/dot_general | solution.py:14
  44.1 1.2 copy.22
  45.3 3.1 %fusion.26 = f32[32,64,128]{2,1,0:T(8,128)} fusion(f32[32,64,128]{2,1,0:T(8,128)S(1)} %copy.22, f32[32,64,64]{2,1,0:T(8,128)S(1)} %get-tuple-element.256, f32[32,64,64]{2,1,0:T(8,128)S(1)} %get-tuple-element.257, f32[32,64,128]{2,1,0:T(8,128)S(1)} %broadcast_select_fusion.3), kind=kOutput, calls=%fused_computation.7.clone.1 | convolution fusion | flops 403701760 | bytes 4194304 | tf_op jit(solution)/shard_map/while/body/eval_jaxpr/bij,bjk->bik/dot_general | solution.py:14
  49.0 1.2 copy.22
  50.2 3.1 %fusion.26 = f32[32,64,128]{2,1,0:T(8,128)} fusion(f32[32,64,128]{2,1,0:T(8,128)S(1)} %copy.22, f32[32,64,64]{2,1,0:T(8,128)S(1)} %get-tuple-element.256, f32[32,64,64]{2,1,0:T(8,128)S(1)} %get-tuple-element.257, f32[32,64,128]{2,1,0:T(8,128)S(1)} %broadcast_select_fusion.3), kind=kOutput, calls=%fused_computation.7.clone.1 | convolution fusion | flops 403701760 | bytes 4194304 | tf_op jit(solution)/shard_map/while/body/eval_jaxpr/bij,bjk->bik/dot_general | solution.py:14
  53.9 1.2 copy.22
  55.1 3.1 %fusion.26 = f32[32,64,128]{2,1,0:T(8,128)} fusion(f32[32,64,128]{2,1,0:T(8,128)S(1)} %copy.22, f32[32,64,64]{2,1,0:T(8,128)S(1)} %get-tuple-element.256, f32[32,64,64]{2,1,0:T(8,128)S(1)} %get-tuple-element.257, f32[32,64,128]{2,1,0:T(8,128)S(1)} %broadcast_select_fusion.3), kind=kOutput, calls=%fused_computation.7.clone.1 | convolution fusion | flops 403701760 | bytes 4194304 | tf_op jit(solution)/shard_map/while/body/eval_jaxpr/bij,bjk->bik/dot_general | solution.py:14
  58.8 1.2 copy.22
  60.0 3.1 %fusion.26 = f32[32,64,128]{2,1,0:T(8,128)} fusion(f32[32,64,128]{2,1,0:T(8,128)S(1)} %copy.22, f32[32,64,64]{2,1,0:T(8,128)S(1)} %get-tuple-element.256, f32[32,64,64]{2,1,0:T(8,128)S(1)} %get-tuple-element.257, f32[32,64,128]{2,1,0:T(8,128)S(1)} %broadcast_select_fusion.3), kind=kOutput, calls=%fused_computation.7.clone.1 | convolution fusion | flops 403701760 | bytes 4194304 | tf_op jit(solution)/shard_map/while/body/eval_jaxpr/bij,bjk->bik/dot_general | solution.py:14
  63.7 1.2 copy.22
  64.9 3.1 %fusion.26 = f32[32,64,128]{2,1,0:T(8,128)} fusion(f32[32,64,128]{2,1,0:T(8,128)S(1)} %copy.22, f32[32,64,64]{2,1,0:T(8,128)S(1)} %get-tuple-element.256, f32[32,64,64]{2,1,0:T(8,128)S(1)} %get-tuple-element.257, f32[32,64,128]{2,1,0:T(8,128)S(1)} %broadcast_select_fusion.3), kind=kOutput, calls=%fused_computation.7.clone.1 | convolution fusion | flops 403701760 | bytes 4194304 | tf_op jit(solution)/shard_map/while/body/eval_jaxpr/bij,bjk->bik/dot_general | solution.py:14
  68.6 1.2 copy.22
  69.8 3.1 %fusion.26 = f32[32,64,128]{2,1,0:T(8,128)} fusion(f32[32,64,128]{2,1,0:T(8,128)S(1)} %copy.22, f32[32,64,64]{2,1,0:T(8,128)S(1)} %get-tuple-element.256, f32[32,64,64]{2,1,0:T(8,128)S(1)} %get-tuple-element.257, f32[32,64,128]{2,1,0:T(8,128)S(1)} %broadcast_select_fusion.3), kind=kOutput, calls=%fused_computation.7.clone.1 | convolution fusion | flops 403701760 | bytes 4194304 | tf_op jit(solution)/shard_map/while/body/eval_jaxpr/bij,bjk->bik/dot_general | solution.py:14
  73.5 1.2 copy.22
  74.7 3.1 %fusion.26 = f32[32,64,128]{2,1,0:T(8,128)} fusion(f32[32,64,128]{2,1,0:T(8,128)S(1)} %copy.22, f32[32,64,64]{2,1,0:T(8,128)S(1)} %get-tuple-element.256, f32[32,64,64]{2,1,0:T(8,128)S(1)} %get-tuple-element.257, f32[32,64,128]{2,1,0:T(8,128)S(1)} %broadcast_select_fusion.3), kind=kOutput, calls=%fused_computation.7.clone.1 | convolution fusion | flops 403701760 | bytes 4194304 | tf_op jit(solution)/shard_map/while/body/eval_jaxpr/bij,bjk->bik/dot_general | solution.py:14
  78.4 1.2 copy.22
  79.6 3.1 %fusion.26 = f32[32,64,128]{2,1,0:T(8,128)} fusion(f32[32,64,128]{2,1,0:T(8,128)S(1)} %copy.22, f32[32,64,64]{2,1,0:T(8,128)S(1)} %get-tuple-element.256, f32[32,64,64]{2,1,0:T(8,128)S(1)} %get-tuple-element.257, f32[32,64,128]{2,1,0:T(8,128)S(1)} %broadcast_select_fusion.3), kind=kOutput, calls=%fused_computation.7.clone.1 | convolution fusion | flops 403701760 | bytes 4194304 | tf_op jit(solution)/shard_map/while/body/eval_jaxpr/bij,bjk->bik/dot_general | solution.py:14
  83.3 1.2 copy.22
  84.5 3.1 %fusion.26 = f32[32,64,128]{2,1,0:T(8,128)} fusion(f32[32,64,128]{2,1,0:T(8,128)S(1)} %copy.22, f32[32,64,64]{2,1,0:T(8,128)S(1)} %get-tuple-element.256, f32[32,64,64]{2,1,0:T(8,128)S(1)} %get-tuple-element.257, f32[32,64,128]{2,1,0:T(8,128)S(1)} %broadcast_select_fusion.3), kind=kOutput, calls=%fused_computation.7.clone.1 | convolution fusion | flops 403701760 | bytes 4194304 | tf_op jit(solution)/shard_map/while/body/eval_jaxpr/bij,bjk->bik/dot_general | solution.py:14
  87.6 6.5 %all-to-all-start = ((f32[4,8,64,128]{3,2,1,0:T(8,128)}), f32[4,8,64,128]{3,2,1,0:T(8,128)S(1)}, u32[]{:S(2)}, u32[]{:S(2)}) async-start(f32[4,8,64,128]{3,2,1,0:T(8,128)} %bitcast.13), calls=%async_computation | async-start | bytes 2097152 | tf_op jit(solution)/shard_map/all_to_all | solution.py:58
  94.2 25.6 %all-to-all-done = f32[4,8,64,128]{3,2,1,0:T(8,128)S(1)} async-done(((f32[4,8,64,128]{3,2,1,0:T(8,128)}), f32[4,8,64,128]{3,2,1,0:T(8,128)S(1)}, u32[]{:S(2)}, u32[]{:S(2)}) %all-to-all-start) | async-done | bytes 1048608 | tf_op jit(solution)/shard_map/all_to_all | solution.py:58
  119.8 3.4 %while.29 = (s32[]{:T(128)}, f32[8,64,128]{2,1,0:T(8,128)S(1)}, f32[4,8,64,128]{3,2,1,0:T(8,128)S(1)}, s32[]{:T(128)}) while((s32[]{:T(128)}, f32[8,64,128]{2,1,0:T(8,128)S(1)}, f32[4,8,64,128]{3,2,1,0:T(8,128)S(1)}, s32[]{:T(128)}) %tuple.74), condition=%wide.region_3.4_spmd, body=%wide.region_2.3_spmd.sunk | while | flops 100958208 | bytes 2621497 | solution.py:61
  120.1 0.6 convolution_bitcast_fusion.2
  120.9 0.6 convolution_bitcast_fusion.2
  121.8 0.6 convolution_bitcast_fusion.2
  122.6 0.6 convolution_bitcast_fusion.2
  123.7 20.2 %psum.7 = f32[2,32]{1,0:T(2,128)} all-reduce(f32[2,32]{1,0:T(2,128)S(1)} %dynamic_update_slice.3), channel_id=1, replica_groups=mesh['grp'=2,'col'=4,'slc'=2,'bat'=2] {'col','slc'}, use_global_device_ids=true, to_apply=%region_6.7 | all-reduce | flops 64 | bytes 512 | tf_op jit(solution)/shard_map/psum | solution.py:73
  (97 shorter events, 10.5 us)
Async XLA Ops:
  0.0 2.5 %copy-start.2 = (s32[32,72]{1,0:T(8,128)S(1)}, s32[32,72]{1,0:T(8,128)}, u32[]{:S(2)}) copy-start(s32[32,72]{1,0:T(8,128)} %param.13) | copy-start | bytes 27652
  87.6 6.5 %copy-start = (f32[1,64,128]{2,1,0:T(8,128)S(1)}, f32[1,64,128]{2,1,0:T(8,128)}, u32[]{:S(2)}) copy-start(f32[1,64,128]{2,1,0:T(8,128)} %param.11) | copy-start | bytes 98308
  87.6 32.2 %copy-start.1 = (f32[1,64,128]{2,1,0:T(8,128)S(1)}, f32[1,64,128]{2,1,0:T(8,128)}, u32[]{:S(2)}) copy-start(f32[1,64,128]{2,1,0:T(8,128)} %param.10) | copy-start | bytes 98308
  87.6 32.2 %all-to-all-start = ((f32[4,8,64,128]{3,2,1,0:T(8,128)}), f32[4,8,64,128]{3,2,1,0:T(8,128)S(1)}, u32[]{:S(2)}, u32[]{:S(2)}) async-start(f32[4,8,64,128]{3,2,1,0:T(8,128)} %bitcast.13), calls=%async_computation | async-start | bytes 2097152 | tf_op jit(solution)/shard_map/all_to_all | solution.py:58
where the time goes:
time: 145 us; the launch traced here: 144 us
  matrix products  55.4 us (38%)
  waiting for transfers between devices  25.6 us (18%)
  local copies, waits for them, and re-layouts  22.1 us (15%)
  blocking collectives  20.2 us (14%)
  other arithmetic  13.5 us (9%)
  starting transfers between devices  6.48 us (4%)
    dot_general x21, matrix products, complex_product(): jnp.einsum('bij,bjk->bik', first_factor, stacked, precision=lax.Precision...  55.4 us
    all_to_all x1, waiting for transfers between devices, on_device(): lax.all_to_all(grouped, 'col', split_axis=0, concat_axis=0, tiled=True)  25.6 us
    while x21, local copies, waits for them, and re-layouts  21 us
    psum x1, blocking collectives, on_device(): return lax.psum(placed, ('col', 'slc'))  20.2 us
    neg x21, other arithmetic, rotate(): return jnp.concatenate([-block[..., middle:], block[..., :middle]], axis=-1)  7.05 us
    all_to_all x1, starting transfers between devices, on_device(): lax.all_to_all(grouped, 'col', split_axis=0, concat_axis=0, tiled=True)  6.48 us
    select_n x18, other arithmetic, select_site(): return jnp.where(chosen_bits[:, None, None] == 1, matrices[1], matrices[0])  3.41 us
  transfers between devices with their start and end apart: 1, of which 1 were waited for; matrix products, arithmetic and copies ran while one was open for 0% of the time, Pallas kernels for 0%

commit v1 on v0

--- a/solution.py
+++ b/solution.py
@@ -70,7 +70,7 @@
     placed = lax.dynamic_update_slice(
         jnp.zeros((2, padded_rows), jnp.float32), closed, (jnp.int32(0), col_index * share)
     )
-    return lax.psum(placed, ("col", "slc"))
+    return lax.psum(lax.psum(placed, "slc"), "col")
 
 
 def solution(mesh):

time: 145 us -> 140 us (0.966)
  blocking collectives: 20.2 us -> 15.4 us
    psum x1 -> x2, blocking collectives: 20.2 us -> 15.4 us  [on_device(): return lax.psum(lax.psum(placed, 'slc'), 'col')]
where the time goes in v1:
time: 140 us; the launch traced here: 139 us
  matrix products  55.6 us (40%)
  waiting for transfers between devices  25.6 us (18%)
  local copies, waits for them, and re-layouts  22.1 us (16%)
  blocking collectives  15.4 us (11%)
  other arithmetic  13.5 us (10%)
  starting transfers between devices  6.48 us (5%)
    dot_general x21, matrix products, complex_product(): jnp.einsum('bij,bjk->bik', first_factor, stacked, precision=lax.Precision...  55.6 us
    all_to_all x1, waiting for transfers between devices, on_device(): lax.all_to_all(grouped, 'col', split_axis=0, concat_axis=0, tiled=True)  25.6 us
    while x21, local copies, waits for them, and re-layouts  21 us
    psum x2, blocking collectives, on_device(): return lax.psum(lax.psum(placed, 'slc'), 'col')  15.4 us
    neg x21, other arithmetic, rotate(): return jnp.concatenate([-block[..., middle:], block[..., :middle]], axis=-1)  7.05 us
    all_to_all x1, starting transfers between devices, on_device(): lax.all_to_all(grouped, 'col', split_axis=0, concat_axis=0, tiled=True)  6.48 us
    select_n x18, other arithmetic, select_site(): return jnp.where(chosen_bits[:, None, None] == 1, matrices[1], matrices[0])  3.42 us
  transfers between devices with their start and end apart: 1, of which 1 were waited for; matrix products, arithmetic and copies ran while one was open for 0% of the time, Pallas kernels for 0%

profile of v1, /device:TPU:0, one launch (start us, length us, event | category | flops | bytes accessed | tf_op | source)
XLA Modules:
  0.0 139.3 jit_solution(13303900282027215822)
XLA Ops:
  0.0 0.7 compare_select_fusion
  0.7 0.7 compare_and_fusion
  1.3 1.2 bitcast_convert_fusion
  3.3 1.1 broadcast_select_fusion.1
  4.4 83.4 %while.28 = (s32[]{:T(128)}, f32[32,64,128]{2,1,0:T(8,128)}, s32[32,18]{0,1:T(8,128)S(1)}, f32[18,2,64,128]{3,2,1,0:T(8,128)S(1)}, s32[]{:T(128)}, /*index=5*/s32[]{:T(128)}, s32[]{:T(128)}, s32[]{}) while((s32[]{:T(128)}, f32[32,64,128]{2,1,0:T(8,128)}, s32[32,18]{0,1:T(8,128)S(1)}, f32[18,2,64,128]{3,2,1,0:T(8,128)S(1)}, s32[]{:T(128)}, ...), condition=%wide.region_1.2_spmd, body=%wide.region_0.1_spmd.sunk | while | flops 404095008 | bytes 9634135 | solution.py:37
  5.0 1.2 copy.22
  6.2 3.1 %fusion.26 = f32[32,64,128]{2,1,0:T(8,128)} fusion(f32[32,64,128]{2,1,0:T(8,128)S(1)} %copy.22, f32[32,64,64]{2,1,0:T(8,128)S(1)} %get-tuple-element.256, f32[32,64,64]{2,1,0:T(8,128)S(1)} %get-tuple-element.257, f32[32,64,128]{2,1,0:T(8,128)S(1)} %broadcast_select_fusion.3), kind=kOutput, calls=%fused_computation.7.clone.1 | convolution fusion | flops 403701760 | bytes 4194304 | tf_op jit(solution)/shard_map/while/body/eval_jaxpr/bij,bjk->bik/dot_general | solution.py:14
  9.9 1.2 copy.22
  11.1 3.1 %fusion.26 = f32[32,64,128]{2,1,0:T(8,128)} fusion(f32[32,64,128]{2,1,0:T(8,128)S(1)} %copy.22, f32[32,64,64]{2,1,0:T(8,128)S(1)} %get-tuple-element.256, f32[32,64,64]{2,1,0:T(8,128)S(1)} %get-tuple-element.257, f32[32,64,128]{2,1,0:T(8,128)S(1)} %broadcast_select_fusion.3), kind=kOutput, calls=%fused_computation.7.clone.1 | convolution fusion | flops 403701760 | bytes 4194304 | tf_op jit(solution)/shard_map/while/body/eval_jaxpr/bij,bjk->bik/dot_general | solution.py:14
  14.8 1.2 copy.22
  16.0 3.1 %fusion.26 = f32[32,64,128]{2,1,0:T(8,128)} fusion(f32[32,64,128]{2,1,0:T(8,128)S(1)} %copy.22, f32[32,64,64]{2,1,0:T(8,128)S(1)} %get-tuple-element.256, f32[32,64,64]{2,1,0:T(8,128)S(1)} %get-tuple-element.257, f32[32,64,128]{2,1,0:T(8,128)S(1)} %broadcast_select_fusion.3), kind=kOutput, calls=%fused_computation.7.clone.1 | convolution fusion | flops 403701760 | bytes 4194304 | tf_op jit(solution)/shard_map/while/body/eval_jaxpr/bij,bjk->bik/dot_general | solution.py:14
  19.7 1.2 copy.22
  20.9 3.1 %fusion.26 = f32[32,64,128]{2,1,0:T(8,128)} fusion(f32[32,64,128]{2,1,0:T(8,128)S(1)} %copy.22, f32[32,64,64]{2,1,0:T(8,128)S(1)} %get-tuple-element.256, f32[32,64,64]{2,1,0:T(8,128)S(1)} %get-tuple-element.257, f32[32,64,128]{2,1,0:T(8,128)S(1)} %broadcast_select_fusion.3), kind=kOutput, calls=%fused_computation.7.clone.1 | convolution fusion | flops 403701760 | bytes 4194304 | tf_op jit(solution)/shard_map/while/body/eval_jaxpr/bij,bjk->bik/dot_general | solution.py:14
  24.6 1.2 copy.22
  25.8 3.1 %fusion.26 = f32[32,64,128]{2,1,0:T(8,128)} fusion(f32[32,64,128]{2,1,0:T(8,128)S(1)} %copy.22, f32[32,64,64]{2,1,0:T(8,128)S(1)} %get-tuple-element.256, f32[32,64,64]{2,1,0:T(8,128)S(1)} %get-tuple-element.257, f32[32,64,128]{2,1,0:T(8,128)S(1)} %broadcast_select_fusion.3), kind=kOutput, calls=%fused_computation.7.clone.1 | convolution fusion | flops 403701760 | bytes 4194304 | tf_op jit(solution)/shard_map/while/body/eval_jaxpr/bij,bjk->bik/dot_general | solution.py:14
  29.5 1.2 copy.22
  30.7 3.1 %fusion.26 = f32[32,64,128]{2,1,0:T(8,128)} fusion(f32[32,64,128]{2,1,0:T(8,128)S(1)} %copy.22, f32[32,64,64]{2,1,0:T(8,128)S(1)} %get-tuple-element.256, f32[32,64,64]{2,1,0:T(8,128)S(1)} %get-tuple-element.257, f32[32,64,128]{2,1,0:T(8,128)S(1)} %broadcast_select_fusion.3), kind=kOutput, calls=%fused_computation.7.clone.1 | convolution fusion | flops 403701760 | bytes 4194304 | tf_op jit(solution)/shard_map/while/body/eval_jaxpr/bij,bjk->bik/dot_general | solution.py:14
  34.4 1.2 copy.22
  35.6 3.1 %fusion.26 = f32[32,64,128]{2,1,0:T(8,128)} fusion(f32[32,64,128]{2,1,0:T(8,128)S(1)} %copy.22, f32[32,64,64]{2,1,0:T(8,128)S(1)} %get-tuple-element.256, f32[32,64,64]{2,1,0:T(8,128)S(1)} %get-tuple-element.257, f32[32,64,128]{2,1,0:T(8,128)S(1)} %broadcast_select_fusion.3), kind=kOutput, calls=%fused_computation.7.clone.1 | convolution fusion | flops 403701760 | bytes 4194304 | tf_op jit(solution)/shard_map/while/body/eval_jaxpr/bij,bjk->bik/dot_general | solution.py:14
  39.3 1.2 copy.22
  40.5 3.1 %fusion.26 = f32[32,64,128]{2,1,0:T(8,128)} fusion(f32[32,64,128]{2,1,0:T(8,128)S(1)} %copy.22, f32[32,64,64]{2,1,0:T(8,128)S(1)} %get-tuple-element.256, f32[32,64,64]{2,1,0:T(8,128)S(1)} %get-tuple-element.257, f32[32,64,128]{2,1,0:T(8,128)S(1)} %broadcast_select_fusion.3), kind=kOutput, calls=%fused_computation.7.clone.1 | convolution fusion | flops 403701760 | bytes 4194304 | tf_op jit(solution)/shard_map/while/body/eval_jaxpr/bij,bjk->bik/dot_general | solution.py:14
  44.2 1.2 copy.22
  45.4 3.1 %fusion.26 = f32[32,64,128]{2,1,0:T(8,128)} fusion(f32[32,64,128]{2,1,0:T(8,128)S(1)} %copy.22, f32[32,64,64]{2,1,0:T(8,128)S(1)} %get-tuple-element.256, f32[32,64,64]{2,1,0:T(8,128)S(1)} %get-tuple-element.257, f32[32,64,128]{2,1,0:T(8,128)S(1)} %broadcast_select_fusion.3), kind=kOutput, calls=%fused_computation.7.clone.1 | convolution fusion | flops 403701760 | bytes 4194304 | tf_op jit(solution)/shard_map/while/body/eval_jaxpr/bij,bjk->bik/dot_general | solution.py:14
  49.1 1.2 copy.22
  50.4 3.1 %fusion.26 = f32[32,64,128]{2,1,0:T(8,128)} fusion(f32[32,64,128]{2,1,0:T(8,128)S(1)} %copy.22, f32[32,64,64]{2,1,0:T(8,128)S(1)} %get-tuple-element.256, f32[32,64,64]{2,1,0:T(8,128)S(1)} %get-tuple-element.257, f32[32,64,128]{2,1,0:T(8,128)S(1)} %broadcast_select_fusion.3), kind=kOutput, calls=%fused_computation.7.clone.1 | convolution fusion | flops 403701760 | bytes 4194304 | tf_op jit(solution)/shard_map/while/body/eval_jaxpr/bij,bjk->bik/dot_general | solution.py:14
  54.0 1.2 copy.22
  55.3 3.1 %fusion.26 = f32[32,64,128]{2,1,0:T(8,128)} fusion(f32[32,64,128]{2,1,0:T(8,128)S(1)} %copy.22, f32[32,64,64]{2,1,0:T(8,128)S(1)} %get-tuple-element.256, f32[32,64,64]{2,1,0:T(8,128)S(1)} %get-tuple-element.257, f32[32,64,128]{2,1,0:T(8,128)S(1)} %broadcast_select_fusion.3), kind=kOutput, calls=%fused_computation.7.clone.1 | convolution fusion | flops 403701760 | bytes 4194304 | tf_op jit(solution)/shard_map/while/body/eval_jaxpr/bij,bjk->bik/dot_general | solution.py:14
  58.9 1.2 copy.22
  60.2 3.1 %fusion.26 = f32[32,64,128]{2,1,0:T(8,128)} fusion(f32[32,64,128]{2,1,0:T(8,128)S(1)} %copy.22, f32[32,64,64]{2,1,0:T(8,128)S(1)} %get-tuple-element.256, f32[32,64,64]{2,1,0:T(8,128)S(1)} %get-tuple-element.257, f32[32,64,128]{2,1,0:T(8,128)S(1)} %broadcast_select_fusion.3), kind=kOutput, calls=%fused_computation.7.clone.1 | convolution fusion | flops 403701760 | bytes 4194304 | tf_op jit(solution)/shard_map/while/body/eval_jaxpr/bij,bjk->bik/dot_general | solution.py:14
  63.8 1.2 copy.22
  65.1 3.1 %fusion.26 = f32[32,64,128]{2,1,0:T(8,128)} fusion(f32[32,64,128]{2,1,0:T(8,128)S(1)} %copy.22, f32[32,64,64]{2,1,0:T(8,128)S(1)} %get-tuple-element.256, f32[32,64,64]{2,1,0:T(8,128)S(1)} %get-tuple-element.257, f32[32,64,128]{2,1,0:T(8,128)S(1)} %broadcast_select_fusion.3), kind=kOutput, calls=%fused_computation.7.clone.1 | convolution fusion | flops 403701760 | bytes 4194304 | tf_op jit(solution)/shard_map/while/body/eval_jaxpr/bij,bjk->bik/dot_general | solution.py:14
  68.7 1.2 copy.22
  70.0 3.1 %fusion.26 = f32[32,64,128]{2,1,0:T(8,128)} fusion(f32[32,64,128]{2,1,0:T(8,128)S(1)} %copy.22, f32[32,64,64]{2,1,0:T(8,128)S(1)} %get-tuple-element.256, f32[32,64,64]{2,1,0:T(8,128)S(1)} %get-tuple-element.257, f32[32,64,128]{2,1,0:T(8,128)S(1)} %broadcast_select_fusion.3), kind=kOutput, calls=%fused_computation.7.clone.1 | convolution fusion | flops 403701760 | bytes 4194304 | tf_op jit(solution)/shard_map/while/body/eval_jaxpr/bij,bjk->bik/dot_general | solution.py:14
  73.7 1.2 copy.22
  74.9 3.1 %fusion.26 = f32[32,64,128]{2,1,0:T(8,128)} fusion(f32[32,64,128]{2,1,0:T(8,128)S(1)} %copy.22, f32[32,64,64]{2,1,0:T(8,128)S(1)} %get-tuple-element.256, f32[32,64,64]{2,1,0:T(8,128)S(1)} %get-tuple-element.257, f32[32,64,128]{2,1,0:T(8,128)S(1)} %broadcast_select_fusion.3), kind=kOutput, calls=%fused_computation.7.clone.1 | convolution fusion | flops 403701760 | bytes 4194304 | tf_op jit(solution)/shard_map/while/body/eval_jaxpr/bij,bjk->bik/dot_general | solution.py:14
  78.6 1.2 copy.22
  79.8 3.1 %fusion.26 = f32[32,64,128]{2,1,0:T(8,128)} fusion(f32[32,64,128]{2,1,0:T(8,128)S(1)} %copy.22, f32[32,64,64]{2,1,0:T(8,128)S(1)} %get-tuple-element.256, f32[32,64,64]{2,1,0:T(8,128)S(1)} %get-tuple-element.257, f32[32,64,128]{2,1,0:T(8,128)S(1)} %broadcast_select_fusion.3), kind=kOutput, calls=%fused_computation.7.clone.1 | convolution fusion | flops 403701760 | bytes 4194304 | tf_op jit(solution)/shard_map/while/body/eval_jaxpr/bij,bjk->bik/dot_general | solution.py:14
  83.5 1.2 copy.22
  84.7 3.1 %fusion.26 = f32[32,64,128]{2,1,0:T(8,128)} fusion(f32[32,64,128]{2,1,0:T(8,128)S(1)} %copy.22, f32[32,64,64]{2,1,0:T(8,128)S(1)} %get-tuple-element.256, f32[32,64,64]{2,1,0:T(8,128)S(1)} %get-tuple-element.257, f32[32,64,128]{2,1,0:T(8,128)S(1)} %broadcast_select_fusion.3), kind=kOutput, calls=%fused_computation.7.clone.1 | convolution fusion | flops 403701760 | bytes 4194304 | tf_op jit(solution)/shard_map/while/body/eval_jaxpr/bij,bjk->bik/dot_general | solution.py:14
  87.8 6.5 %all-to-all-start = ((f32[4,8,64,128]{3,2,1,0:T(8,128)}), f32[4,8,64,128]{3,2,1,0:T(8,128)S(1)}, u32[]{:S(2)}, u32[]{:S(2)}) async-start(f32[4,8,64,128]{3,2,1,0:T(8,128)} %bitcast.13), calls=%async_computation | async-start | bytes 2097152 | tf_op jit(solution)/shard_map/all_to_all | solution.py:58
  94.4 25.6 %all-to-all-done = f32[4,8,64,128]{3,2,1,0:T(8,128)S(1)} async-done(((f32[4,8,64,128]{3,2,1,0:T(8,128)}), f32[4,8,64,128]{3,2,1,0:T(8,128)S(1)}, u32[]{:S(2)}, u32[]{:S(2)}) %all-to-all-start) | async-done | bytes 1048608 | tf_op jit(solution)/shard_map/all_to_all | solution.py:58
  120.1 3.4 %while.29 = (s32[]{:T(128)}, f32[8,64,128]{2,1,0:T(8,128)S(1)}, f32[4,8,64,128]{3,2,1,0:T(8,128)S(1)}, s32[]{:T(128)}) while((s32[]{:T(128)}, f32[8,64,128]{2,1,0:T(8,128)S(1)}, f32[4,8,64,128]{3,2,1,0:T(8,128)S(1)}, s32[]{:T(128)}) %tuple.74), condition=%wide.region_3.4_spmd, body=%wide.region_2.3_spmd.sunk | while | flops 100958208 | bytes 2621497 | solution.py:61
  120.3 0.6 convolution_bitcast_fusion.2
  121.1 0.6 convolution_bitcast_fusion.2
  122.0 0.6 convolution_bitcast_fusion.2
  122.8 0.6 convolution_bitcast_fusion.2
  123.9 4.9 %psum.14 = f32[2,32]{1,0:T(2,128)S(1)} all-reduce(f32[2,32]{1,0:T(2,128)S(1)} %dynamic_update_slice.3), channel_id=1, replica_groups=mesh['grp'=2,'col'=4,'slc'=2,'bat'=2] {'slc'}, use_global_device_ids=true, to_apply=%region_6.7 | all-reduce | flops 64 | bytes 512 | tf_op jit(solution)/shard_map/psum | solution.py:73
  128.8 10.5 %psum.15 = f32[2,32]{1,0:T(2,128)} all-reduce(f32[2,32]{1,0:T(2,128)S(1)} %psum.14), channel_id=1, replica_groups=mesh['grp'=2,'col'=4,'slc'=2,'bat'=2] {'col'}, use_global_device_ids=true, to_apply=%region_7.8 | all-reduce | flops 64 | bytes 512 | tf_op jit(solution)/shard_map/psum | solution.py:73
  (98 shorter events, 11.0 us)
Async XLA Ops:
  0.0 2.5 %copy-start.2 = (s32[32,72]{1,0:T(8,128)S(1)}, s32[32,72]{1,0:T(8,128)}, u32[]{:S(2)}) copy-start(s32[32,72]{1,0:T(8,128)} %param.13) | copy-start | bytes 27652
  87.8 6.5 %copy-start = (f32[1,64,128]{2,1,0:T(8,128)S(1)}, f32[1,64,128]{2,1,0:T(8,128)}, u32[]{:S(2)}) copy-start(f32[1,64,128]{2,1,0:T(8,128)} %param.11) | copy-start | bytes 98308
  87.8 32.2 %copy-start.1 = (f32[1,64,128]{2,1,0:T(8,128)S(1)}, f32[1,64,128]{2,1,0:T(8,128)}, u32[]{:S(2)}) copy-start(f32[1,64,128]{2,1,0:T(8,128)} %param.10) | copy-start | bytes 98308
  87.8 32.2 %all-to-all-start = ((f32[4,8,64,128]{3,2,1,0:T(8,128)}), f32[4,8,64,128]{3,2,1,0:T(8,128)S(1)}, u32[]{:S(2)}, u32[]{:S(2)}) async-start(f32[4,8,64,128]{3,2,1,0:T(8,128)} %bitcast.13), calls=%async_computation | async-start | bytes 2097152 | tf_op jit(solution)/shard_map/all_to_all | solution.py:58
